TPU v7x, 32 devices: a whole 2x2x4 slice. The times are simulated.
32 devices in a mesh: gx: 8 (over z, x), gy: 4 (over y, core).
Axes of the slice: x: 2, y: 2, z: 4, core: 2. Of those that a mesh axis runs over, the one named last changes fastest.
Arguments:
- state: float32 [65536, 128], P(('gx', 'gy')), may hold values from 0 to 1
- velocity: bfloat16 [3, 3, 128, 64, 128], P(None, None, 'gx', 'gy'), may hold values from -3 to 3
- cells: int32 [3, 3, 65536], P(None, None, ('gx', 'gy')), may hold values from -1 to 126, as said below
- slots: int32 [3, 65536], P(None, ('gx', 'gy')), may hold values from 0 to 2047, as said below
- counts: int32 [3, 8, 4, 8], P(None, 'gx', 'gy'), may hold values from 0 to 64, as said below
Outputs:
- final_state: float32 [65536, 128], P(('gx', 'gy'))
Inputs may be any that keep to these rules, and one draw needn't show every extreme that they name: For every section and device the 2048 values of slots are a permutation of 0 to 2047. counts[s, i, j, r] equals counts[s, i', j', r xor 1] where (i', j') is the neighbour of (i, j) in direction r; some device sends exactly 64 in every section. cells[s, 0] lies in -1 to 15, cells[s, 1] in -1 to 15, cells[s, 2] in 0 to 126.
All inputs are finite; a program needn't handle non-finite values.
Results may differ from a plain program's by a relative error of at most 0.0003.
Values may be sent and summed in bfloat16 or wider, within the bound.
A program may use at most 64 MiB of HBM per device.

v0:
```python
import functools

import jax
import jax.numpy as jnp
from jax import lax
from jax.experimental import pallas as pl
from jax.experimental.pallas import tpu as pltpu
from jax.sharding import PartitionSpec as P

GAMMA = (8.0 / 15.0, 5.0 / 12.0, 3.0 / 4.0)
ZETA = (0.0, -17.0 / 60.0, -5.0 / 12.0)
OFFSETS = ((1, 0), (-1, 0), (0, 1), (0, -1), (1, 1), (-1, -1), (1, -1), (-1, 1))
SPARE = 8
BLOCK = 512
MESH = pl.DeviceIdType.MESH
VMEM = pl.BlockSpec(memory_space=pltpu.VMEM)
SMEM = pl.BlockSpec(memory_space=pltpu.SMEM)


def neighbour(r, sizes):
    off_x, off_y = OFFSETS[r]
    i, j = lax.axis_index("gx"), lax.axis_index("gy")
    return (lax.rem(i + off_x + sizes[0], sizes[0]), lax.rem(j + off_y + sizes[1], sizes[1]))


def greet(sizes):
    barrier = pltpu.get_barrier_semaphore()
    for r in range(8):
        pl.semaphore_signal(barrier, inc=1, device_id=neighbour(r, sizes), device_id_type=MESH)
    pl.semaphore_wait(barrier, 8)


def send(r, src, dst, sems, group, sizes):
    copy = pltpu.make_async_remote_copy(
        src_ref=src,
        dst_ref=dst,
        send_sem=sems[0].at[group, r],
        recv_sem=sems[1].at[group, r ^ 1],
        device_id=neighbour(r, sizes),
        device_id_type=MESH,
    )
    copy.start()
    return copy


def parts_of(x):
    high = x.astype(jnp.bfloat16)
    rest = x - high.astype(jnp.float32)
    middle = rest.astype(jnp.bfloat16)
    low = (rest - middle.astype(jnp.float32)).astype(jnp.bfloat16)
    return high, middle, low


def cell_weights(size, cell, frac):
    spots = lax.broadcasted_iota(jnp.int32, (size, cell.shape[1]), 0)
    low, high = 1.0 - frac, frac
    inside = jnp.where(spots == cell, low, 0.0) + jnp.where(spots == cell + 1, high, 0.0)
    return inside, jnp.where(cell == -1, low, 0.0), jnp.where(cell == size - 1, high, 0.0)


def gather_rows(order_ref, section, source_ref, leave_ref, cap):
    first = section * 8 * cap

    def body(step, carry):
        for u in range(16):
            t = step * 16 + u
            leave_ref[section, pl.ds(t, 1), :] = source_ref[pl.ds(order_ref[first + t], 1), :]
        return carry

    lax.fori_loop(0, 8 * cap // 16, body, 0)


def build_onehot(slot_ref, section, onehot_ref):
    slot = slot_ref[section]
    moving = slot.shape[1]
    step_rows = 256

    def body(step, carry):
        base = pl.multiple_of(step * step_rows, step_rows)
        spots = lax.broadcasted_iota(jnp.int32, (step_rows, moving), 0) + base
        onehot_ref[pl.ds(base, step_rows), :] = jnp.where(spots == slot, 1.0, 0.0).astype(jnp.bfloat16)
        return carry

    lax.fori_loop(0, onehot_ref.shape[0] // step_rows, body, 0)


def build_plane(section, dims, v_ref, halo_ref, corner_ref, plane_ref):
    cx, cy = dims
    inner = cx * cy
    depth = v_ref.shape[3]
    for k in range(3):
        row = 3 * section + k
        own = v_ref[row].reshape(inner, depth)
        plane_ref[pl.ds(k * depth, depth), 0:inner] = own.T
        faces = halo_ref[row].astype(jnp.float32)
        corners = [corner_ref[d, row : row + 1, :] for d in range(4)]
        filler = jnp.zeros((128 - faces.shape[0] - 4, depth), jnp.float32)
        edge = jnp.concatenate([faces] + corners + [filler], axis=0)
        width = plane_ref.shape[1] - inner
        plane_ref[pl.ds(k * depth, depth), inner:] = edge.T[:, 0:width].astype(jnp.bfloat16)


def sample(section, dims, head, cell, plane_ref):
    cx, cy = dims
    depth = plane_ref.shape[0] // 3
    block = head.shape[1]
    wx, wx_low, wx_high = cell_weights(cx, cell[0:1], head[0:1])
    wy, wy_low, wy_high = cell_weights(cy, cell[1:2], head[1:2])
    wz, _, _ = cell_weights(depth, cell[2:3], head[2:3])
    parts = [wx[x : x + 1] * wy for x in range(cx)]
    parts += [wx_high * wy, wx_low * wy, wx * wy_high, wx * wy_low]
    parts += [wx_high * wy_high, wx_low * wy_low, wx_high * wy_low, wx_low * wy_high]
    parts += [jnp.zeros((12, block), jnp.float32)]
    whole = jnp.concatenate(parts, axis=0)
    high = whole.astype(jnp.bfloat16)
    low = (whole - high.astype(jnp.float32)).astype(jnp.bfloat16)
    columns = jnp.dot(plane_ref[...], high, preferred_element_type=jnp.float32)
    columns = columns + jnp.dot(plane_ref[...], low, preferred_element_type=jnp.float32)
    speed = jnp.concatenate(
        [jnp.sum(columns[k * depth : (k + 1) * depth] * wz, axis=0, keepdims=True) for k in range(3)],
        axis=0,
    )
    moved = head[0:3] + GAMMA[section] * speed + ZETA[section] * head[3:6]
    return jnp.concatenate([moved, speed, jnp.ones((2, block), jnp.float32)], axis=0)


def sample_all(section, dims, cells_ref, head_ref, plane_ref):
    block = BLOCK

    def body(step, carry):
        span = pl.ds(pl.multiple_of(step * block, block), block)
        head_ref[:, span] = sample(section, dims, head_ref[:, span], cells_ref[section, :, span], plane_ref)
        return carry

    lax.fori_loop(0, head_ref.shape[1] // block, body, 0)


def plan_kernel(cap, slots_ref, counts_ref, v_ref, index_ref, slot_ref, taken_ref, yface_ref, away_ref):
    sections, count = slots_ref.shape
    moving = 8 * cap
    fields, inner, depth = v_ref.shape
    cx = yface_ref.shape[2]
    cy = inner // cx
    lanes = lax.broadcasted_iota(jnp.int32, (1, moving), 1)
    within = lax.rem(lanes, cap)
    places = lax.broadcasted_iota(jnp.int32, (moving, moving), 0) + count
    chunks = moving // 128
    columns = []
    for section in range(sections):
        slot = slots_ref[section : section + 1, 0:moving]
        limit = jnp.zeros((1, moving), jnp.int32)
        for r in range(8):
            limit = jnp.where(lanes >= r * cap, counts_ref[section, 0, 0, r], limit)
        taken = within < limit
        goal = jnp.where(taken, slot, count)
        found = jnp.full((1, moving), -1, jnp.int32)
        for past in range(section):
            match = columns[past] == slot
            best = jnp.max(jnp.where(match, places, -1), axis=0, keepdims=True)
            found = jnp.where(best >= 0, best + past * moving, found)
        source = jnp.where(found >= 0, found, slot)
        if section + 1 < sections:
            wide = jnp.broadcast_to(goal.astype(jnp.float32), (8, moving))
            columns.append(wide.T[:, 0:1].astype(jnp.int32))
        slot_ref[section] = slot
        taken_ref[section] = jnp.where(taken, 1.0, 0.0)
        for c in range(chunks):
            span = slice(c * 128, (c + 1) * 128)
            row = section * chunks + c
            index_ref[row : row + 1, :] = source[:, span]
            row += sections * chunks
            index_ref[row : row + 1, :] = goal[:, span]
    row = lax.broadcasted_iota(jnp.int32, (2 * cx + 8, inner), 0)
    place = lax.broadcasted_iota(jnp.int32, (2 * cx + 8, inner), 1)
    want = jnp.where(row < cx, row * cy + cy - 1, (row - cx) * cy)
    for d, spot in enumerate((inner - 1, 0, (cx - 1) * cy, cy - 1)):
        want = jnp.where(row == 2 * cx + d, spot, want)
    pick = jnp.where(want == place, 1.0, 0.0).astype(jnp.bfloat16)
    for f in range(fields):
        edge = jnp.dot(pick, v_ref[f], preferred_element_type=jnp.float32)
        yface_ref[0, f] = edge[0:cx].astype(jnp.bfloat16)
        yface_ref[1, f] = edge[cx : 2 * cx].astype(jnp.bfloat16)
        for d in range(4):
            away_ref[d, f : f + 1, :] = edge[2 * cx + d : 2 * cx + d + 1]


def steps_kernel(
    sizes,
    cap,
    order_ref,
    slot_ref,
    taken_ref,
    cells_ref,
    v_ref,
    yface_ref,
    away_ref,
    state_ref,
    head_ref,
    arrived_ref,
    rows_ref,
    leave_ref,
    onehot_ref,
    plane_ref,
    halo_ref,
    corner_ref,
    head_out_ref,
    head_in_ref,
    send_sem,
    recv_sem,
):
    sems = (send_sem, recv_sem)
    sections = slot_ref.shape[0]
    cx, cy = v_ref.shape[1], v_ref.shape[2]
    count = state_ref.shape[0]
    moving = 8 * cap
    starts = (0, cy, 2 * cy, 2 * cy + cx)
    widths = (cy, cy, cx, cx)
    greet(sizes)

    halos = []
    for section in range(sections):
        group = []
        fields = pl.ds(3 * section, 3)
        for r in range(4):
            off_x, off_y = OFFSETS[r]
            src = v_ref.at[fields, cx - 1 if off_x > 0 else 0] if off_x else yface_ref.at[r - 2, fields]
            dst = halo_ref.at[fields, pl.ds(starts[r ^ 1], widths[r ^ 1]), :]
            group.append(send(r, src, dst, sems, section, sizes))
        if section == 0:
            for r in range(4, 8):
                group.append(send(r, away_ref.at[r - 4], corner_ref.at[(r ^ 1) - 4], sems, section, sizes))
        halos.append(group)

    def send_rows(section):
        gather_rows(order_ref, section, rows_ref, leave_ref, cap)
        return [
            send(
                r,
                leave_ref.at[section, pl.ds(r * cap, cap)],
                arrived_ref.at[pl.ds(section * moving + (r ^ 1) * cap, cap)],
                sems,
                sections + section,
                sizes,
            )
            for r in range(8)
        ]

    rows_ref[0:count, :] = state_ref[...]
    carried = send_rows(0)
    for b in range(count // 128):
        head_ref[:, b * 128 : (b + 1) * 128] = state_ref[b * 128 : (b + 1) * 128, :].T[0:8]
    for section in range(sections):
        if section == 0:
            build_onehot(slot_ref, 0, onehot_ref.at[0])
        hot = onehot_ref.at[section % 2]
        where_ = cells_ref[section].astype(jnp.float32)
        stacked = [part.astype(jnp.float32) for part in parts_of(head_ref[...])] + [where_]
        stacked = jnp.concatenate(stacked, axis=0).astype(jnp.bfloat16)
        picked = jnp.dot(stacked, hot[...], preferred_element_type=jnp.float32)
        leaving = picked[0:8] + picked[8:16] + picked[16:24]
        there = picked[24:27].astype(jnp.int32)
        for copy in halos[section]:
            copy.wait()
        build_plane(section, (cx, cy), v_ref, halo_ref, corner_ref, plane_ref)
        leaving = jnp.concatenate(
            [
                sample(section, (cx, cy), leaving[:, b : b + BLOCK], there[:, b : b + BLOCK], plane_ref)
                for b in range(0, moving, BLOCK)
            ],
            axis=1,
        )
        heads = []
        for r in range(8):
            head_out_ref[section, r] = leaving[:, r * cap : (r + 1) * cap]
        for r in range(8):
            heads.append(
                send(
                    r,
                    head_out_ref.at[section, r],
                    head_in_ref.at[section, r ^ 1],
                    sems,
                    2 * sections + section,
                    sizes,
                )
            )
        sample_all(section, (cx, cy), cells_ref, head_ref, plane_ref)
        for copy in carried:
            copy.wait()
        if section + 1 < sections:
            low = section * moving
            rows_ref[count + low : count + low + moving, :] = arrived_ref[low : low + moving, :]
            carried = send_rows(section + 1)
            build_onehot(slot_ref, section + 1, onehot_ref.at[(section + 1) % 2])
        for copy in heads:
            copy.wait()
        came = jnp.concatenate([head_in_ref[section, r] for r in range(8)], axis=1)
        came = came * taken_ref[section]
        stacked = jnp.concatenate([part.astype(jnp.float32) for part in parts_of(came)], axis=0)
        spread = lax.dot_general(
            stacked.astype(jnp.bfloat16), hot[...], (((1,), (1,)), ((), ())), preferred_element_type=jnp.float32
        )
        placed = spread[0:8] + spread[8:16] + spread[16:24]
        head_ref[...] = jnp.where(placed[6:7] > 0.5, placed, head_ref[...])


def last_kernel(offset, index_ref, state_ref, arrived_ref, head_ref, out_ref, rows_ref):
    count, width = out_ref.shape
    rows_ref[0:count, :] = state_ref[...]

    def body(step, carry):
        for u in range(16):
            t = step * 16 + u
            rows_ref[pl.ds(index_ref[offset + t], 1), :] = arrived_ref[pl.ds(t, 1), :]
        return carry

    lax.fori_loop(0, arrived_ref.shape[0] // 16, body, 0)
    lanes = lax.broadcasted_iota(jnp.int32, (128, width), 1)
    for b in range(count // 128):
        span = slice(b * 128, (b + 1) * 128)
        full = jnp.concatenate([head_ref[:, span], jnp.zeros((width - 8, 128), jnp.float32)], axis=0)
        out_ref[span, :] = jnp.where(lanes < 6, full.T, rows_ref[span, :])


def local(sizes, cap, state, velocity, cells, slots, counts):
    sections, _, cx, cy, depth = velocity.shape
    count, width = state.shape
    moving = 8 * cap
    fields = sections * 3
    field = velocity.reshape(fields, cx, cy, depth)
    rows = 2 * sections * moving // 128
    rows += -rows % 8
    edges = (4, fields + -fields % 8, depth)
    index, slot, taken, yface, away = pl.pallas_call(
        functools.partial(plan_kernel, cap),
        out_shape=(
            jax.ShapeDtypeStruct((rows, 128), jnp.int32),
            jax.ShapeDtypeStruct((sections, 1, moving), jnp.int32),
            jax.ShapeDtypeStruct((sections, 1, moving), jnp.float32),
            jax.ShapeDtypeStruct((2, fields, cx, depth), field.dtype),
            jax.ShapeDtypeStruct(edges, jnp.float32),
        ),
        in_specs=[VMEM, SMEM, VMEM],
        out_specs=(VMEM,) * 5,
    )(slots, counts, field.reshape(fields, cx * cy, depth))
    index = index.reshape(rows * 128)

    head, arrived = pl.pallas_call(
        functools.partial(steps_kernel, sizes, cap),
        out_shape=(
            jax.ShapeDtypeStruct((8, count), jnp.float32),
            jax.ShapeDtypeStruct((sections * moving, width), jnp.float32),
        ),
        in_specs=[SMEM] + [VMEM] * 7,
        out_specs=(VMEM, VMEM),
        scratch_shapes=[
            pltpu.VMEM((count + (sections - 1) * moving, width), jnp.float32),
            pltpu.VMEM((sections, moving, width), jnp.float32),
            pltpu.VMEM((2, count, moving), jnp.bfloat16),
            pltpu.VMEM((3 * depth, cx * cy + 2 * cx + 2 * cy + 16), jnp.bfloat16),
            pltpu.VMEM((fields, 2 * cx + 2 * cy, depth), jnp.bfloat16),
            pltpu.VMEM(edges, jnp.float32),
            pltpu.VMEM((sections, 8, 8, cap), jnp.float32),
            pltpu.VMEM((sections, 8, 8, cap), jnp.float32),
            pltpu.SemaphoreType.DMA((3 * sections, 8)),
            pltpu.SemaphoreType.DMA((3 * sections, 8)),
        ],
        compiler_params=pltpu.CompilerParams(collective_id=0, has_side_effects=True),
    )(
        index,
        slot,
        taken,
        cells,
        field,
        yface,
        away,
        state,
    )
    return pl.pallas_call(
        functools.partial(last_kernel, sections * moving),
        out_shape=jax.ShapeDtypeStruct((count, width), jnp.float32),
        in_specs=[SMEM, VMEM, VMEM, VMEM],
        out_specs=VMEM,
        scratch_shapes=[pltpu.VMEM((count + SPARE, width), jnp.float32)],
    )(index, state, arrived, head)


def solution(mesh):
    return jax.shard_map(
        functools.partial(local, (mesh.shape["gx"], mesh.shape["gy"]), 64),
        mesh=mesh,
        in_specs=(
            P(("gx", "gy"), None),
            P(None, None, "gx", "gy", None),
            P(None, None, ("gx", "gy")),
            P(None, ("gx", "gy")),
            P(None, "gx", "gy", None),
        ),
        out_specs=P(("gx", "gy"), None),
        check_vma=False,
    )
```

profile of v0, /device:TPU:0, one launch (start us, length us, event | category | flops | bytes accessed | tf_op | source)
XLA Modules:
  0.0 39.0 jit_solution(10537660783445938965)
XLA Ops:
  0.0 2.5 %shard_map.55 = (s32[24,128]{1,0:T(8,128)}, s32[3,1,512]{2,1,0:T(1,128)}, f32[3,1,512]{2,1,0:T(1,128)}, bf16[2,9,16,128]{3,2,1,0:T(8,128)(2,1)}, f32[4,16,128]{2,1,0:T(8,128)}) custom-call(s32[3,2048]{1,0:T(4,128)} %slots_ref.1, s32[3,1,1,8]{3,2,1,0:T(1,128)} %counts_ref.1, bf16[9,256,128]{2,1,0:T(8,128)(2,1)} %bitcast.3), custom_call_target="tpu_custom_call" | custom-call | tf_op jit(solution)/shard_map/pallas_call | solution.py:333
  2.5 32.0 %shard_map.56 = (f32[8,2048]{1,0:T(8,128)}, f32[1536,128]{1,0:T(8,128)}) custom-call(s32[3072]{0:T(1024)} %bitcast.5, s32[3,1,512]{2,1,0:T(1,128)} %get-tuple-element.13.slot_ref, f32[3,1,512]{2,1,0:T(1,128)} %get-tuple-element.14.taken_ref, s32[3,3,2048]{2,1,0:T(4,128)} %cells_ref.1, bf16[9,16,16,128]{3,2,1,0:T(8,128)(2,1)} %bitcast.4, ...), custom_call_target="tpu_custom_call" | custom-call | tf_op jit(solution)/shard_map/pallas_call | solution.py:347
  34.5 4.5 %shard_map.57 = f32[2048,128]{1,0:T(8,128)} custom-call(s32[3072]{0:T(1024)} %bitcast.6, f32[2048,128]{1,0:T(8,128)} %state_ref.3, f32[1536,128]{1,0:T(8,128)} %get-tuple-element.17.arrived_ref, f32[8,2048]{1,0:T(8,128)} %get-tuple-element.18.head_ref), custom_call_target="tpu_custom_call" | custom-call | tf_op jit(solution)/shard_map/pallas_call | solution.py:378
where the time goes:
time: 39.3 us; the launch traced here: 39 us
  Pallas kernels  39 us (99%)
    pallas_call x1, Pallas kernels, local(): pl.pallas_call(functools.partial(steps_kernel, sizes, cap), out_shape=(ja...  32 us
    pallas_call x1, Pallas kernels, local(): pl.pallas_call(functools.partial(last_kernel, sections * moving), out_sha...  4.52 us
    pallas_call x1, Pallas kernels, local(): pl.pallas_call(functools.partial(plan_kernel, cap), out_shape=(jax.ShapeD...  2.53 us

commit v1 on v0

v1 whole, which is shorter than its diff:
```python
import functools

import jax
import jax.numpy as jnp
from jax import lax
from jax.experimental import pallas as pl
from jax.experimental.pallas import tpu as pltpu
from jax.sharding import PartitionSpec as P

GAMMA = (8.0 / 15.0, 5.0 / 12.0, 3.0 / 4.0)
ZETA = (0.0, -17.0 / 60.0, -5.0 / 12.0)
OFFSETS = ((1, 0), (-1, 0), (0, 1), (0, -1), (1, 1), (-1, -1), (1, -1), (-1, 1))
LANES = 128
SPARE = 8
BLOCK = 512
MESH = pl.DeviceIdType.MESH
VMEM = pl.BlockSpec(memory_space=pltpu.VMEM)
SMEM = pl.BlockSpec(memory_space=pltpu.SMEM)
ANY = pl.BlockSpec(memory_space=pl.ANY)


def neighbour(r, sizes):
    off_x, off_y = OFFSETS[r]
    i, j = lax.axis_index("gx"), lax.axis_index("gy")
    return (lax.rem(i + off_x + sizes[0], sizes[0]), lax.rem(j + off_y + sizes[1], sizes[1]))


def send(r, src, dst, sems, group, sizes):
    copy = pltpu.make_async_remote_copy(
        src_ref=src,
        dst_ref=dst,
        send_sem=sems[0].at[group, r],
        recv_sem=sems[1].at[group, r],
        device_id=neighbour(r, sizes),
        device_id_type=MESH,
    )
    copy.start()
    return copy


def tile(x, k):
    return x[:, k * LANES : (k + 1) * LANES]


def spread_row(row):
    return jnp.broadcast_to(row, (8, LANES))


def select_lanes(tiles, where_, start):
    low, high = where_ & (LANES - 1), where_ >> 7
    out = start
    for k, source in enumerate(tiles):
        out = jnp.where(high == k, jnp.take_along_axis(source, low, axis=1), out)
    return out


def look_up(table, where_):
    low, high = spread_row(where_ & (LANES - 1)), spread_row(where_ >> 7)
    row = lax.broadcasted_iota(jnp.int32, (8, LANES), 0)
    best = jnp.zeros((8, LANES), jnp.int32)
    for g in range(table.shape[0] // 8):
        got = jnp.take_along_axis(table[8 * g : 8 * g + 8], low, axis=1)
        best = jnp.where(row + 8 * g == high, got, best)
    return jnp.max(best, axis=0, keepdims=True)


def cell_weights(size, cell, frac):
    spots = lax.broadcasted_iota(jnp.int32, (size, cell.shape[1]), 0)
    low, high = 1.0 - frac, frac
    inside = jnp.where(spots == cell, low, jnp.where(spots == cell + 1, high, 0.0))
    return inside, jnp.where(cell == -1, low, 0.0), jnp.where(cell == size - 1, high, 0.0)


def halves(whole):
    high = whole.astype(jnp.bfloat16)
    return high, (whole - high.astype(jnp.float32)).astype(jnp.bfloat16)


def sample(section, dims, head, cell, plane_ref):
    cx, cy = dims
    inner = cx * cy
    depth = plane_ref.shape[0] // 3
    block = head.shape[1]
    wx, wx_low, wx_high = cell_weights(cx, cell[0:1], head[0:1])
    wy, wy_low, wy_high = cell_weights(cy, cell[1:2], head[1:2])
    wz, _, _ = cell_weights(depth, cell[2:3], head[2:3])
    own = jnp.concatenate([wx[x : x + 1] * wy for x in range(cx)], axis=0)
    rim = [wx_high * wy, wx_low * wy, wx * wy_high, wx * wy_low]
    rim += [wx_high * wy_high, wx_low * wy_low, wx_high * wy_low, wx_low * wy_high]
    rim += [jnp.zeros((LANES - 2 * cx - 2 * cy - 4, block), jnp.float32)]
    own_high, own_low = halves(own)
    rim = jnp.concatenate(halves(jnp.concatenate(rim, axis=0)), axis=0)
    inside = plane_ref[:, 0:inner]
    columns = jnp.dot(inside, own_high, preferred_element_type=jnp.float32)
    columns = columns + jnp.dot(inside, own_low, preferred_element_type=jnp.float32)
    columns = columns + jnp.dot(plane_ref[:, inner:], rim, preferred_element_type=jnp.float32)
    speed = jnp.concatenate(
        [jnp.sum(columns[k * depth : (k + 1) * depth] * wz, axis=0, keepdims=True) for k in range(3)],
        axis=0,
    )
    moved = head[0:3] + GAMMA[section] * speed + ZETA[section] * head[3:6]
    return jnp.concatenate([moved, speed, jnp.ones((2, block), jnp.float32)], axis=0)


def sample_all(section, dims, cells_ref, head_ref, plane_ref):
    block = BLOCK

    def body(step, carry):
        span = pl.ds(pl.multiple_of(step * block, block), block)
        head_ref[:, span] = sample(section, dims, head_ref[:, span], cells_ref[section, :, span], plane_ref)
        return carry

    lax.fori_loop(0, head_ref.shape[1] // block, body, 0)


def gather_rows(index_ref, section, source_ref, leave_ref):
    def body(row, carry):
        for u in range(LANES):
            leave_ref[section, pl.ds(row * LANES + u, 1), :] = source_ref[pl.ds(index_ref[section, row, u], 1), :]
        return carry

    lax.fori_loop(0, leave_ref.shape[1] // LANES, body, 0)


def find_edges(fields, dims, v_ref, yface_ref, away_ref):
    cx, cy = dims
    inner = cx * cy
    row = lax.broadcasted_iota(jnp.int32, (2 * cx + 8, inner), 0)
    place = lax.broadcasted_iota(jnp.int32, (2 * cx + 8, inner), 1)
    want = jnp.where(row < cx, row * cy + cy - 1, (row - cx) * cy)
    for d, spot in enumerate((inner - 1, 0, (cx - 1) * cy, cy - 1)):
        want = jnp.where(row == 2 * cx + d, spot, want)
    pick = jnp.where(want == place, 1.0, 0.0).astype(jnp.bfloat16)
    for f in fields:
        edge = jnp.dot(pick, v_ref[f].reshape(inner, v_ref.shape[3]), preferred_element_type=jnp.float32)
        yface_ref[0, f] = edge[0:cx].astype(jnp.bfloat16)
        yface_ref[1, f] = edge[cx : 2 * cx].astype(jnp.bfloat16)
        group, line = (0, f) if f < 3 else (1, f - 3)
        for d in range(4):
            away_ref[group, d, line : line + 1, :] = edge[2 * cx + d : 2 * cx + d + 1]


def build_inside(section, dims, v_ref, plane_ref):
    inner = dims[0] * dims[1]
    depth = v_ref.shape[3]
    for k in range(3):
        own = v_ref[3 * section + k].reshape(inner, depth)
        plane_ref[pl.ds(k * depth, depth), 0:inner] = own.T


def build_rim(section, dims, halo_ref, corner_ref, plane_ref):
    inner = dims[0] * dims[1]
    depth = halo_ref.shape[2]
    for k in range(3):
        f = 3 * section + k
        group, line = (0, f) if f < 3 else (1, f - 3)
        faces = halo_ref[f].astype(jnp.float32)
        corners = [corner_ref[group, d, line : line + 1, :] for d in range(4)]
        filler = jnp.zeros((LANES - faces.shape[0] - 4, depth), jnp.float32)
        edge = jnp.concatenate([faces] + corners + [filler], axis=0).T.astype(jnp.bfloat16)
        plane_ref[pl.ds(k * depth, depth), inner : inner + LANES] = edge
        plane_ref[pl.ds(k * depth, depth), inner + LANES :] = edge


def plan(section, cap, count, slots_ref, counts_ref):
    moving = 8 * cap
    blocks = count // LANES
    slot = slots_ref[section : section + 1, 0:moving]
    lanes = lax.broadcasted_iota(jnp.int32, (1, moving), 1)
    limit = jnp.zeros((1, moving), jnp.int32)
    for r in range(8):
        limit = jnp.where(lanes >= r * cap, counts_ref[section, 0, 0, r], limit)
    taken = lax.rem(lanes, cap) < limit
    goal = jnp.where(taken, slot, count)
    value = jnp.where(taken, (lanes ^ cap) + 1, 0)
    low, high = slot & (LANES - 1), slot >> 7
    line = lax.broadcasted_iota(jnp.int32, (blocks, moving), 0)
    upper = jnp.where(line == high, (value >> 5).astype(jnp.float32), 0.0)
    lower = jnp.where(line == high, (value & 31).astype(jnp.float32), 0.0)
    left = jnp.concatenate([upper, lower], axis=0).astype(jnp.bfloat16)
    spots = lax.broadcasted_iota(jnp.int32, (LANES, moving), 0)
    right = jnp.where(spots == low, 1.0, 0.0).astype(jnp.bfloat16)
    both = lax.dot_general(left, right, (((1,), (1,)), ((), ())), preferred_element_type=jnp.float32)
    inverse = (both[0:blocks] * 32.0 + both[blocks:]).astype(jnp.int32)
    return slot, goal, inverse


def steps_kernel(
    sizes,
    cap,
    state_hbm,
    v_hbm,
    cells_hbm,
    slots_hbm,
    counts_hbm,
    rows_ref,
    arrived_ref,
    head_ref,
    index_ref,
    counts_ref,
    v_ref,
    cells_ref,
    slots_ref,
    staged_ref,
    inverse_ref,
    from_ref,
    there_ref,
    own_ref,
    leave_ref,
    plane_ref,
    yface_ref,
    away_ref,
    halo_ref,
    corner_ref,
    head_out_ref,
    head_in_ref,
    local_sem,
    send_sem,
    recv_sem,
):
    sems = (send_sem, recv_sem)
    sections, _, count = cells_ref.shape
    cx, cy = v_ref.shape[1], v_ref.shape[2]
    dims = (cx, cy)
    moving = 8 * cap
    chunks = moving // LANES
    blocks = count // LANES
    fields = 3 * sections
    starts = (0, cy, 2 * cy, 2 * cy + cx)
    widths = (cy, cy, cx, cx)

    barrier = pltpu.get_barrier_semaphore()
    for r in range(8):
        pl.semaphore_signal(barrier, inc=1, device_id=neighbour(r, sizes), device_id_type=MESH)

    def fetch(k, src, dst):
        copy = pltpu.make_async_copy(src, dst, local_sem.at[k])
        copy.start()
        return copy

    load_first = fetch(0, v_hbm.at[pl.ds(0, 3)], v_ref.at[pl.ds(0, 3)])
    load_slots = fetch(1, slots_hbm, slots_ref)
    load_counts = fetch(2, counts_hbm, counts_ref)
    load_state = fetch(3, state_hbm, rows_ref.at[pl.ds(0, count)])
    load_cells = fetch(4, cells_hbm, cells_ref)
    load_rest = fetch(5, v_hbm.at[pl.ds(3, fields - 3)], v_ref.at[pl.ds(3, fields - 3)])

    def send_halo(group):
        span = pl.ds(0, 3) if group == 0 else pl.ds(3, fields - 3)
        copies = []
        for r in range(8):
            if r < 4:
                off_x, off_y = OFFSETS[r]
                src = v_ref.at[span, cx - 1 if off_x > 0 else 0] if off_x else yface_ref.at[r - 2, span]
                dst = halo_ref.at[span, pl.ds(starts[r ^ 1], widths[r ^ 1]), :]
            else:
                src, dst = away_ref.at[group, r - 4], corner_ref.at[group, (r ^ 1) - 4]
            copies.append(send(r, src, dst, sems, group, sizes))
        return copies

    load_first.wait()
    find_edges(range(3), dims, v_ref, yface_ref, away_ref)
    pl.semaphore_wait(barrier, 8)
    halos = [send_halo(0)]

    load_slots.wait()
    load_counts.wait()
    slots, inverses = [], []
    table = lax.broadcasted_iota(jnp.int32, (blocks, LANES), 0) * LANES
    table = table + lax.broadcasted_iota(jnp.int32, (blocks, LANES), 1)
    places = []
    for section in range(sections):
        slot, goal, inverse = plan(section, cap, count, slots_ref, counts_ref)
        if section:
            packed = table * 1024 + inverses[-1]
            found = [look_up(packed, tile(slot, c)) for c in range(chunks)]
            for c in range(chunks):
                staged_ref[section, c : c + 1, :] = jnp.clip(found[c] >> 10, 0, count + section * moving - 1)
                from_ref[section, c : c + 1, :] = (found[c] & 1023) - 1
        else:
            for c in range(chunks):
                staged_ref[section, c : c + 1, :] = tile(slot, c)
        for c in range(chunks):
            staged_ref[section, chunks + c : chunks + c + 1, :] = tile(goal, c)
        places.append(fetch(6 + section, staged_ref.at[section], index_ref.at[section]))
        table = jnp.where(inverse > 0, inverse + (count + section * moving - 1), table)
        inverse_ref[section] = inverse - 1
        slots.append(slot)
        inverses.append(inverse)

    load_rest.wait()
    find_edges(range(3, fields), dims, v_ref, yface_ref, away_ref)
    halos.append(send_halo(1))

    def send_rows(section):
        places[section].wait()
        gather_rows(index_ref, section, rows_ref, leave_ref)
        return [
            send(
                r,
                leave_ref.at[section, pl.ds(r * cap, cap)],
                arrived_ref.at[pl.ds(section * moving + r * cap, cap)],
                sems,
                2 + section,
                sizes,
            )
            for r in range(8)
        ]

    load_state.wait()
    carried = [send_rows(0)]
    build_inside(0, dims, v_ref, plane_ref.at[0])
    for b in range(blocks):
        head_ref[:, b * LANES : (b + 1) * LANES] = rows_ref[b * LANES : (b + 1) * LANES, :].T[0:8]

    load_cells.wait()
    line = lax.broadcasted_iota(jnp.int32, (8, LANES), 0)
    packed = []
    for b in range(blocks):
        span = slice(b * LANES, (b + 1) * LANES)
        both = jnp.zeros((8, LANES), jnp.int32)
        for section in range(sections):
            spot = cells_ref[section, :, span]
            word = (spot[0:1] + 1) + (spot[1:2] + 1) * 1024 + spot[2:3] * 1048576
            both = jnp.where(line == section, spread_row(word), both)
        packed.append(both)
    for c in range(chunks):
        where_ = spread_row(tile(slots[0], c))
        for section in range(1, sections):
            where_ = jnp.where(line == section, spread_row(tile(slots[section], c)), where_)
        there_ref[c] = select_lanes(packed, where_, jnp.zeros((8, LANES), jnp.int32))

    def pick_own(section):
        tiles = [head_ref[:, b * LANES : (b + 1) * LANES] for b in range(blocks)]
        for c in range(chunks):
            where_ = spread_row(slots_ref[section : section + 1, c * LANES : (c + 1) * LANES])
            own_ref[c] = select_lanes(tiles, where_, jnp.zeros((8, LANES), jnp.float32))

    def arrivals(section):
        first = lax.broadcasted_iota(jnp.int32, (8, LANES), 1) < cap
        return [
            jnp.where(first, head_in_ref[section, 2 * c], head_in_ref[section, 2 * c + 1]) for c in range(chunks)
        ]

    pick_own(0)
    heads = []
    for section in range(sections):
        if section == 0:
            for copy in halos[0]:
                copy.wait_recv()
            build_rim(0, dims, halo_ref, corner_ref, plane_ref.at[0])
            leaving = [own_ref[c] for c in range(chunks)]
        else:
            for copy in heads[section - 1]:
                copy.wait_recv()
            came = arrivals(section - 1)
            leaving = [
                select_lanes(came, spread_row(from_ref[section, c : c + 1, :]), own_ref[c]) for c in range(chunks)
            ]
        word = jnp.concatenate([there_ref[c, section : section + 1, :] for c in range(chunks)], axis=1)
        spot = jnp.concatenate([(word & 1023) - 1, ((word >> 10) & 1023) - 1, word >> 20], axis=0)
        leaving = sample(section, dims, jnp.concatenate(leaving, axis=1), spot, plane_ref.at[section])
        for c in range(chunks):
            head_out_ref[section, c] = tile(leaving, c)
        heads.append(
            [
                send(r, head_out_ref.at[section, r // 2], head_in_ref.at[section, r], sems, 2 + sections + section, sizes)
                for r in range(8)
            ]
        )

        if section:
            place_arrivals(section - 1, arrivals(section - 1), inverse_ref, head_ref)
        sample_all(section, dims, cells_ref, head_ref, plane_ref.at[section])
        if section + 1 < sections:
            pick_own(section + 1)
            build_inside(section + 1, dims, v_ref, plane_ref.at[section + 1])
            if section == 0:
                for copy in halos[1]:
                    copy.wait_recv()
            build_rim(section + 1, dims, halo_ref, corner_ref, plane_ref.at[section + 1])
            for copy in carried[section]:
                copy.wait_recv()
            low = section * moving
            rows_ref[count + low : count + low + moving, :] = arrived_ref[low : low + moving, :]
            carried.append(send_rows(section + 1))

    for copy in carried[sections - 1]:
        copy.wait_recv()
    for copy in heads[sections - 1]:
        copy.wait_recv()
    place_arrivals(sections - 1, arrivals(sections - 1), inverse_ref, head_ref)
    for copies in halos + carried + heads:
        for copy in copies:
            copy.wait_send()


def place_arrivals(section, came, inverse_ref, head_ref):
    for b in range(head_ref.shape[1] // LANES):
        span = slice(b * LANES, (b + 1) * LANES)
        where_ = spread_row(inverse_ref[section, b : b + 1, :])
        head_ref[:, span] = select_lanes(came, where_, head_ref[:, span])


def last_kernel(cap, rows_ref, arrived_ref, head_ref, index_ref, out_ref, final_ref):
    count, width = out_ref.shape
    sections = index_ref.shape[0]
    moving = 8 * cap
    chunks = moving // LANES
    final_ref[0:count, :] = rows_ref[0:count, :]
    for section in range(sections):

        def body(row, carry):
            first = section * moving + row * LANES
            for u in range(LANES):
                goal = index_ref[section, chunks + row, u]
                final_ref[pl.ds(goal, 1), :] = arrived_ref[pl.ds(first + (u ^ cap), 1), :]
            return carry

        lax.fori_loop(0, chunks, body, 0)
    lanes = lax.broadcasted_iota(jnp.int32, (LANES, width), 1)
    for b in range(count // LANES):
        span = slice(b * LANES, (b + 1) * LANES)
        full = jnp.concatenate([head_ref[:, span], jnp.zeros((width - 8, LANES), jnp.float32)], axis=0)
        out_ref[span, :] = jnp.where(lanes < 6, full.T, final_ref[span, :])


def local(sizes, cap, state, velocity, cells, slots, counts):
    sections, _, cx, cy, depth = velocity.shape
    count, width = state.shape
    moving = 8 * cap
    chunks = moving // LANES
    fields = sections * 3
    field = velocity.reshape(fields, cx, cy, depth)
    inner = cx * cy
    rim = 2 * cx + 2 * cy
    rows, arrived, head, index, _ = pl.pallas_call(
        functools.partial(steps_kernel, sizes, cap),
        out_shape=(
            pltpu.VMEM((count + (sections - 1) * moving, width), jnp.float32),
            pltpu.VMEM((sections * moving, width), jnp.float32),
            pltpu.VMEM((8, count), jnp.float32),
            pltpu.SMEM((sections, 2 * chunks, LANES), jnp.int32),
            pltpu.SMEM(counts.shape, jnp.int32),
        ),
        in_specs=[ANY] * 5,
        out_specs=(VMEM, VMEM, VMEM, SMEM, SMEM),
        scratch_shapes=[
            pltpu.VMEM(field.shape, field.dtype),
            pltpu.VMEM(cells.shape, jnp.int32),
            pltpu.VMEM(slots.shape, jnp.int32),
            pltpu.VMEM((sections, 2 * chunks, LANES), jnp.int32),
            pltpu.VMEM((sections, count // LANES, LANES), jnp.int32),
            pltpu.VMEM((sections, chunks, LANES), jnp.int32),
            pltpu.VMEM((chunks, 8, LANES), jnp.int32),
            pltpu.VMEM((chunks, 8, LANES), jnp.float32),
            pltpu.VMEM((sections, moving, width), jnp.float32),
            pltpu.VMEM((sections, 3 * depth, inner + 2 * LANES), jnp.bfloat16),
            pltpu.VMEM((2, fields, cx, depth), field.dtype),
            pltpu.VMEM((2, 4, 8, depth), jnp.float32),
            pltpu.VMEM((fields, rim, depth), field.dtype),
            pltpu.VMEM((2, 4, 8, depth), jnp.float32),
            pltpu.VMEM((sections, chunks, 8, LANES), jnp.float32),
            pltpu.VMEM((sections, 8, 8, LANES), jnp.float32),
            pltpu.SemaphoreType.DMA((6 + sections,)),
            pltpu.SemaphoreType.DMA((2 + 2 * sections, 8)),
            pltpu.SemaphoreType.DMA((2 + 2 * sections, 8)),
        ],
        compiler_params=pltpu.CompilerParams(collective_id=0, has_side_effects=True),
    )(state, field, cells, slots, counts)
    rows, arrived, head = (pltpu.with_memory_space_constraint(x, pltpu.VMEM) for x in (rows, arrived, head))
    index = pltpu.with_memory_space_constraint(index, pltpu.SMEM)
    return pl.pallas_call(
        functools.partial(last_kernel, cap),
        out_shape=jax.ShapeDtypeStruct((count, width), jnp.float32),
        in_specs=[VMEM, VMEM, VMEM, SMEM],
        out_specs=VMEM,
        scratch_shapes=[pltpu.VMEM((count + SPARE, width), jnp.float32)],
    )(rows, arrived, head, index)


def solution(mesh):
    return jax.shard_map(
        functools.partial(local, (mesh.shape["gx"], mesh.shape["gy"]), 64),
        mesh=mesh,
        in_specs=(
            P(("gx", "gy"), None),
            P(None, None, "gx", "gy", None),
            P(None, None, ("gx", "gy")),
            P(None, ("gx", "gy")),
            P(None, "gx", "gy", None),
        ),
        out_specs=P(("gx", "gy"), None),
        check_vma=False,
    )
```

time: 39.3 us -> 31.9 us (0.81)
  Pallas kernels: 39 us -> 31.7 us
    pallas_call x3 -> x2, Pallas kernels: 39 us -> 31.7 us  [the longest x1 29.1 us: local(): pl.pallas_call(functools.partial(steps_kernel, sizes, cap), out_shape=(pl...]
where the time goes in v1:
time: 31.9 us; the launch traced here: 31.7 us
  Pallas kernels  31.7 us (99%)
    pallas_call x1, Pallas kernels, local(): pl.pallas_call(functools.partial(steps_kernel, sizes, cap), out_shape=(pl...  29.1 us
    pallas_call x1, Pallas kernels, local(): pl.pallas_call(functools.partial(last_kernel, cap), out_shape=jax.ShapeDt...  2.59 us

profile of v1, /device:TPU:0, one launch (start us, length us, event | category | flops | bytes accessed | tf_op | source)
XLA Modules:
  0.0 31.7 jit_solution(10531154039007450364)
XLA Ops:
  0.0 29.1 %shard_map.55 = (f32[3072,128]{1,0:T(8,128)S(1)}, f32[1536,128]{1,0:T(8,128)S(1)}, f32[8,2048]{1,0:T(8,128)S(1)}, s32[3,8,128]{2,1,0:T(8,128)S(4)}, s32[3,1,1,8]{3,2,1,0:T(1,128)S(4)}) custom-call(f32[2048,128]{1,0:T(8,128)} %state_hbm.1, bf16[9,16,16,128]{3,2,1,0:T(8,128)(2,1)} %bitcast.1, s32[3,3,2048]{2,1,0:T(4,128)} %cells_hbm.1, s32[3,2048]{1,0:T(4,128)} %slots_hbm.1, ...), custom_call_target="tpu_custom_call" | custom-call | tf_op jit(solution)/shard_map/pallas_call | solution.py:437
  29.1 2.6 %shard_map.56 = f32[2048,128]{1,0:T(8,128)} custom-call(f32[3072,128]{1,0:T(8,128)S(1)} %get-tuple-element.9.rows_ref, f32[1536,128]{1,0:T(8,128)S(1)} %get-tuple-element.10.arrived_ref, f32[8,2048]{1,0:T(8,128)S(1)} %get-tuple-element.11.head_ref, s32[3,8,128]{2,1,0:T(8,128)S(4)} %get-tuple-element.12.index_ref), custom_call_target="tpu_custom_call" | custom-call | tf_op jit(solution)/shard_map/pallas_call | solution.py:473

commit v2 on v1

--- a/solution.py
+++ b/solution.py
@@ -12,6 +12,7 @@
 OFFSETS = ((1, 0), (-1, 0), (0, 1), (0, -1), (1, 1), (-1, -1), (1, -1), (-1, 1))
 LANES = 128
 SPARE = 8
+TOP = 65535.0
 BLOCK = 512
 MESH = pl.DeviceIdType.MESH
 VMEM = pl.BlockSpec(memory_space=pltpu.VMEM)
@@ -26,16 +27,25 @@
 
 
 def send(r, src, dst, sems, group, sizes):
-    copy = pltpu.make_async_remote_copy(
+    pltpu.make_async_remote_copy(
         src_ref=src,
         dst_ref=dst,
-        send_sem=sems[0].at[group, r],
-        recv_sem=sems[1].at[group, r],
+        send_sem=sems[0].at[group],
+        recv_sem=sems[1].at[group],
         device_id=neighbour(r, sizes),
         device_id_type=MESH,
+    ).start()
+
+
+def whole(everything, sems, group, sizes):
+    return pltpu.make_async_remote_copy(
+        src_ref=everything,
+        dst_ref=everything,
+        send_sem=sems[0].at[group],
+        recv_sem=sems[1].at[group],
+        device_id=neighbour(0, sizes),
+        device_id_type=MESH,
     )
-    copy.start()
-    return copy
 
 
 def tile(x, k):
@@ -71,9 +81,9 @@
     return inside, jnp.where(cell == -1, low, 0.0), jnp.where(cell == size - 1, high, 0.0)
 
 
-def halves(whole):
-    high = whole.astype(jnp.bfloat16)
-    return high, (whole - high.astype(jnp.float32)).astype(jnp.bfloat16)
+def halves(value):
+    high = value.astype(jnp.bfloat16)
+    return high, (value - high.astype(jnp.float32)).astype(jnp.bfloat16)
 
 
 def sample(section, dims, head, cell, plane_ref):
@@ -113,13 +123,43 @@
     lax.fori_loop(0, head_ref.shape[1] // block, body, 0)
 
 
-def gather_rows(index_ref, section, source_ref, leave_ref):
+def gather_rows(index_ref, source_ref, target_ref):
     def body(row, carry):
         for u in range(LANES):
-            leave_ref[section, pl.ds(row * LANES + u, 1), :] = source_ref[pl.ds(index_ref[section, row, u], 1), :]
+            target_ref[pl.ds(row * LANES + u, 1), :] = source_ref[pl.ds(index_ref[row, u], 1), :]
         return carry
 
-    lax.fori_loop(0, leave_ref.shape[1] // LANES, body, 0)
+    lax.fori_loop(0, target_ref.shape[0] // LANES, body, 0)
+
+
+def encode(rows):
+    lane = lax.broadcasted_iota(jnp.int32, rows.shape, 1)
+    top = jnp.max(jnp.where(lane < 6, 0.0, rows), axis=1, keepdims=True)
+    power = jnp.clip(jnp.floor(-jnp.log2(top)), 0.0, 100.0)
+    code = jnp.minimum(rows * (jnp.exp2(power) * TOP) + 0.5, TOP)
+    return jnp.where(lane < 6, power, code).astype(jnp.int32)
+
+
+def decode(code):
+    value = code.astype(jnp.float32)
+    return value * (jnp.exp2(-value[:, 0:1]) * (1.0 / TOP))
+
+
+def encode_rows(leave_ref, packed_ref):
+    half = packed_ref.shape[0] // 8
+    for r in range(8):
+        first = encode(leave_ref[2 * half * r : 2 * half * r + half, :])
+        second = encode(leave_ref[2 * half * r + half : 2 * half * (r + 1), :])
+        packed_ref[half * r : half * (r + 1), :] = (first << 16) | second
+
+
+def decode_rows(packed_ref, target_ref, start):
+    half = packed_ref.shape[0] // 8
+    for r in range(8):
+        word = packed_ref[half * r : half * (r + 1), :]
+        low = start + 2 * half * r
+        target_ref[low : low + half, :] = decode((word >> 16) & 65535)
+        target_ref[low + half : low + 2 * half, :] = decode(word & 65535)
 
 
 def find_edges(fields, dims, v_ref, yface_ref, away_ref):
@@ -193,15 +233,20 @@
     cells_hbm,
     slots_hbm,
     counts_hbm,
+    base_ref,
+    merged_ref,
+    index_ref,
+    counts_ref,
+    places_ref,
     rows_ref,
+    packed_ref,
     arrived_ref,
     head_ref,
-    index_ref,
-    counts_ref,
     v_ref,
     cells_ref,
     slots_ref,
     staged_ref,
+    final_ref,
     inverse_ref,
     from_ref,
     there_ref,
@@ -245,18 +290,22 @@
     load_cells = fetch(4, cells_hbm, cells_ref)
     load_rest = fetch(5, v_hbm.at[pl.ds(3, fields - 3)], v_ref.at[pl.ds(3, fields - 3)])
 
+    spans = (pl.ds(0, 3), pl.ds(3, fields - 3))
+
     def send_halo(group):
-        span = pl.ds(0, 3) if group == 0 else pl.ds(3, fields - 3)
-        copies = []
+        span = spans[group]
         for r in range(8):
             if r < 4:
                 off_x, off_y = OFFSETS[r]
                 src = v_ref.at[span, cx - 1 if off_x > 0 else 0] if off_x else yface_ref.at[r - 2, span]
                 dst = halo_ref.at[span, pl.ds(starts[r ^ 1], widths[r ^ 1]), :]
+                send(r, src, dst, sems, 2 * group, sizes)
             else:
                 src, dst = away_ref.at[group, r - 4], corner_ref.at[group, (r ^ 1) - 4]
-            copies.append(send(r, src, dst, sems, group, sizes))
-        return copies
+                send(r, src, dst, sems, 2 * group + 1, sizes)
+        faces = whole(halo_ref.at[span], sems, 2 * group, sizes)
+        corners = whole(corner_ref.at[group], sems, 2 * group + 1, sizes)
+        return [faces, corners]
 
     load_first.wait()
     find_edges(range(3), dims, v_ref, yface_ref, away_ref)
@@ -283,6 +332,9 @@
         for c in range(chunks):
             staged_ref[section, chunks + c : chunks + c + 1, :] = tile(goal, c)
         places.append(fetch(6 + section, staged_ref.at[section], index_ref.at[section]))
+        if section + 1 == sections:
+            final_ref[...] = jnp.clip(table, 0, count + section * moving - 1)
+            places.append(fetch(6 + sections, final_ref, places_ref))
         table = jnp.where(inverse > 0, inverse + (count + section * moving - 1), table)
         inverse_ref[section] = inverse - 1
         slots.append(slot)
@@ -294,18 +346,13 @@
 
     def send_rows(section):
         places[section].wait()
-        gather_rows(index_ref, section, rows_ref, leave_ref)
-        return [
-            send(
-                r,
-                leave_ref.at[section, pl.ds(r * cap, cap)],
-                arrived_ref.at[pl.ds(section * moving + r * cap, cap)],
-                sems,
-                2 + section,
-                sizes,
-            )
-            for r in range(8)
-        ]
+        gather_rows(index_ref.at[section], rows_ref, leave_ref)
+        encode_rows(leave_ref, packed_ref.at[section])
+        half = cap // 2
+        for r in range(8):
+            span = pl.ds(r * half, half)
+            send(r, packed_ref.at[section, span], arrived_ref.at[section, span], sems, 4 + section, sizes)
+        return [whole(arrived_ref.at[section], sems, 4 + section, sizes)]
 
     load_state.wait()
     carried = [send_rows(0)]
@@ -362,12 +409,10 @@
         leaving = sample(section, dims, jnp.concatenate(leaving, axis=1), spot, plane_ref.at[section])
         for c in range(chunks):
             head_out_ref[section, c] = tile(leaving, c)
-        heads.append(
-            [
-                send(r, head_out_ref.at[section, r // 2], head_in_ref.at[section, r], sems, 2 + sections + section, sizes)
-                for r in range(8)
-            ]
-        )
+        group = 4 + sections + section
+        for r in range(8):
+            send(r, head_out_ref.at[section, r // 2], head_in_ref.at[section, r], sems, group, sizes)
+        heads.append([whole(head_in_ref.at[section], sems, group, sizes)])
 
         if section:
             place_arrivals(section - 1, arrivals(section - 1), inverse_ref, head_ref)
@@ -381,18 +426,33 @@
             build_rim(section + 1, dims, halo_ref, corner_ref, plane_ref.at[section + 1])
             for copy in carried[section]:
                 copy.wait_recv()
-            low = section * moving
-            rows_ref[count + low : count + low + moving, :] = arrived_ref[low : low + moving, :]
+            decode_rows(arrived_ref.at[section], rows_ref, count + section * moving)
             carried.append(send_rows(section + 1))
 
+    places[sections].wait()
+    gather_rows(places_ref, rows_ref, base_ref)
+    for b in range(blocks):
+        span = slice(b * LANES, (b + 1) * LANES)
+        base_ref[span, :] = merge_head(head_ref[:, span], base_ref[span, :])
     for copy in carried[sections - 1]:
         copy.wait_recv()
+    decode_rows(arrived_ref.at[sections - 1], merged_ref, 0)
+    for copies in halos + carried + heads[:-1]:
+        for copy in copies:
+            copy.wait_send()
     for copy in heads[sections - 1]:
         copy.wait_recv()
-    place_arrivals(sections - 1, arrivals(sections - 1), inverse_ref, head_ref)
-    for copies in halos + carried + heads:
-        for copy in copies:
-            copy.wait_send()
+    for c, came in enumerate(arrivals(sections - 1)):
+        span = slice(c * LANES, (c + 1) * LANES)
+        merged_ref[span, :] = merge_head(came, merged_ref[span, :])
+    for copy in heads[sections - 1]:
+        copy.wait_send()
+
+
+def merge_head(head, rows):
+    lane = lax.broadcasted_iota(jnp.int32, rows.shape, 1)
+    full = jnp.concatenate([head, jnp.zeros((rows.shape[1] - 8, LANES), jnp.float32)], axis=0)
+    return jnp.where(lane < 6, full.T, rows)
 
 
 def place_arrivals(section, came, inverse_ref, head_ref):
@@ -402,27 +462,22 @@
         head_ref[:, span] = select_lanes(came, where_, head_ref[:, span])
 
 
-def last_kernel(cap, rows_ref, arrived_ref, head_ref, index_ref, out_ref, final_ref):
-    count, width = out_ref.shape
-    sections = index_ref.shape[0]
-    moving = 8 * cap
-    chunks = moving // LANES
-    final_ref[0:count, :] = rows_ref[0:count, :]
-    for section in range(sections):
-
-        def body(row, carry):
-            first = section * moving + row * LANES
-            for u in range(LANES):
-                goal = index_ref[section, chunks + row, u]
-                final_ref[pl.ds(goal, 1), :] = arrived_ref[pl.ds(first + (u ^ cap), 1), :]
-            return carry
-
-        lax.fori_loop(0, chunks, body, 0)
-    lanes = lax.broadcasted_iota(jnp.int32, (LANES, width), 1)
-    for b in range(count // LANES):
-        span = slice(b * LANES, (b + 1) * LANES)
-        full = jnp.concatenate([head_ref[:, span], jnp.zeros((width - 8, LANES), jnp.float32)], axis=0)
-        out_ref[span, :] = jnp.where(lanes < 6, full.T, final_ref[span, :])
+def last_kernel(cap, base_ref, merged_ref, index_ref, out_hbm, final_ref, sem):
+    count = out_hbm.shape[0]
+    last = index_ref.shape[0] - 1
+    chunks = 8 * cap // LANES
+    final_ref[0:count, :] = base_ref[...]
+
+    def body(row, carry):
+        for u in range(LANES):
+            goal = index_ref[last, chunks + row, u]
+            final_ref[pl.ds(goal, 1), :] = merged_ref[pl.ds(row * LANES + (u ^ cap), 1), :]
+        return carry
+
+    lax.fori_loop(0, chunks, body, 0)
+    copy = pltpu.make_async_copy(final_ref.at[pl.ds(0, count)], out_hbm, sem)
+    copy.start()
+    copy.wait()
 
 
 def local(sizes, cap, state, velocity, cells, slots, counts):
@@ -434,27 +489,33 @@
     field = velocity.reshape(fields, cx, cy, depth)
     inner = cx * cy
     rim = 2 * cx + 2 * cy
-    rows, arrived, head, index, _ = pl.pallas_call(
+    half = moving // 2
+    base, merged, index, _, _ = pl.pallas_call(
         functools.partial(steps_kernel, sizes, cap),
         out_shape=(
-            pltpu.VMEM((count + (sections - 1) * moving, width), jnp.float32),
-            pltpu.VMEM((sections * moving, width), jnp.float32),
-            pltpu.VMEM((8, count), jnp.float32),
+            pltpu.VMEM((count, width), jnp.float32),
+            pltpu.VMEM((moving, width), jnp.float32),
             pltpu.SMEM((sections, 2 * chunks, LANES), jnp.int32),
             pltpu.SMEM(counts.shape, jnp.int32),
+            pltpu.SMEM((count // LANES, LANES), jnp.int32),
         ),
         in_specs=[ANY] * 5,
-        out_specs=(VMEM, VMEM, VMEM, SMEM, SMEM),
+        out_specs=(VMEM, VMEM, SMEM, SMEM, SMEM),
         scratch_shapes=[
+            pltpu.VMEM((count + (sections - 1) * moving, width), jnp.float32),
+            pltpu.VMEM((sections, half, width), jnp.int32),
+            pltpu.VMEM((sections, half, width), jnp.int32),
+            pltpu.VMEM((8, count), jnp.float32),
             pltpu.VMEM(field.shape, field.dtype),
             pltpu.VMEM(cells.shape, jnp.int32),
             pltpu.VMEM(slots.shape, jnp.int32),
             pltpu.VMEM((sections, 2 * chunks, LANES), jnp.int32),
+            pltpu.VMEM((count // LANES, LANES), jnp.int32),
             pltpu.VMEM((sections, count // LANES, LANES), jnp.int32),
             pltpu.VMEM((sections, chunks, LANES), jnp.int32),
             pltpu.VMEM((chunks, 8, LANES), jnp.int32),
             pltpu.VMEM((chunks, 8, LANES), jnp.float32),
-            pltpu.VMEM((sections, moving, width), jnp.float32),
+            pltpu.VMEM((moving, width), jnp.float32),
             pltpu.VMEM((sections, 3 * depth, inner + 2 * LANES), jnp.bfloat16),
             pltpu.VMEM((2, fields, cx, depth), field.dtype),
             pltpu.VMEM((2, 4, 8, depth), jnp.float32),
@@ -462,21 +523,21 @@
             pltpu.VMEM((2, 4, 8, depth), jnp.float32),
             pltpu.VMEM((sections, chunks, 8, LANES), jnp.float32),
             pltpu.VMEM((sections, 8, 8, LANES), jnp.float32),
-            pltpu.SemaphoreType.DMA((6 + sections,)),
-            pltpu.SemaphoreType.DMA((2 + 2 * sections, 8)),
-            pltpu.SemaphoreType.DMA((2 + 2 * sections, 8)),
+            pltpu.SemaphoreType.DMA((7 + sections,)),
+            pltpu.SemaphoreType.DMA((4 + 2 * sections,)),
+            pltpu.SemaphoreType.DMA((4 + 2 * sections,)),
         ],
         compiler_params=pltpu.CompilerParams(collective_id=0, has_side_effects=True),
     )(state, field, cells, slots, counts)
-    rows, arrived, head = (pltpu.with_memory_space_constraint(x, pltpu.VMEM) for x in (rows, arrived, head))
+    base, merged = (pltpu.with_memory_space_constraint(x, pltpu.VMEM) for x in (base, merged))
     index = pltpu.with_memory_space_constraint(index, pltpu.SMEM)
     return pl.pallas_call(
         functools.partial(last_kernel, cap),
         out_shape=jax.ShapeDtypeStruct((count, width), jnp.float32),
-        in_specs=[VMEM, VMEM, VMEM, SMEM],
-        out_specs=VMEM,
-        scratch_shapes=[pltpu.VMEM((count + SPARE, width), jnp.float32)],
-    )(rows, arrived, head, index)
+        in_specs=[VMEM, VMEM, SMEM],
+        out_specs=ANY,
+        scratch_shapes=[pltpu.VMEM((count + SPARE, width), jnp.float32), pltpu.SemaphoreType.DMA],
+    )(base, merged, index)
 
 
 def solution(mesh):

time: 31.9 us -> 27.6 us (0.87)
  Pallas kernels: 31.7 us -> 27.1 us
    pallas_call x1, Pallas kernels: 29.1 us -> 25.7 us  [local(): pl.pallas_call(functools.partial(steps_kernel, sizes, cap), out_shape=(pl...]
    pallas_call x1, Pallas kernels: 2.59 us -> 1.47 us  [local(): pl.pallas_call(functools.partial(last_kernel, cap), out_shape=jax.ShapeDt...]
where the time goes in v2:
time: 27.6 us; the launch traced here: 27.1 us
  Pallas kernels  27.1 us (98%)
    pallas_call x1, Pallas kernels, local(): pl.pallas_call(functools.partial(steps_kernel, sizes, cap), out_shape=(pl...  25.7 us
    pallas_call x1, Pallas kernels, local(): pl.pallas_call(functools.partial(last_kernel, cap), out_shape=jax.ShapeDt...  1.47 us

profile of v2, /device:TPU:0, one launch (start us, length us, event | category | flops | bytes accessed | tf_op | source)
XLA Modules:
  0.0 27.1 jit_solution(4250940242031370075)
XLA Ops:
  0.0 25.7 %shard_map.55 = (f32[2048,128]{1,0:T(8,128)S(1)}, f32[512,128]{1,0:T(8,128)S(1)}, s32[3,8,128]{2,1,0:T(8,128)S(4)}, s32[3,1,1,8]{3,2,1,0:T(1,128)S(4)}, s32[16,128]{1,0:T(8,128)S(4)}) custom-call(f32[2048,128]{1,0:T(8,128)} %state_hbm.1, bf16[9,16,16,128]{3,2,1,0:T(8,128)(2,1)} %bitcast.1, s32[3,3,2048]{2,1,0:T(4,128)} %cells_hbm.1, s32[3,2048]{1,0:T(4,128)} %slots_hbm.1, ...), custom_call_target="tpu_custom_call" | custom-call | tf_op jit(solution)/shard_map/pallas_call | solution.py:493
  25.7 1.5 %shard_map.56 = f32[2048,128]{1,0:T(8,128)} custom-call(f32[2048,128]{1,0:T(8,128)S(1)} %get-tuple-element.8.base_ref, f32[512,128]{1,0:T(8,128)S(1)} %get-tuple-element.9.merged_ref, s32[3,8,128]{2,1,0:T(8,128)S(4)} %get-tuple-element.10.index_ref), custom_call_target="tpu_custom_call" | custom-call | tf_op jit(solution)/shard_map/pallas_call | solution.py:534

commit v3 on v2

--- a/solution.py
+++ b/solution.py
@@ -11,6 +11,8 @@
 ZETA = (0.0, -17.0 / 60.0, -5.0 / 12.0)
 OFFSETS = ((1, 0), (-1, 0), (0, 1), (0, -1), (1, 1), (-1, -1), (1, -1), (-1, 1))
 LANES = 128
+FAR = ((0, 2), (0, -2))
+CORNER_SLOT = (2, 0, 3, 1)
 SPARE = 8
 TOP = 65535.0
 BLOCK = 512
@@ -20,19 +22,19 @@
 ANY = pl.BlockSpec(memory_space=pl.ANY)
 
 
-def neighbour(r, sizes):
-    off_x, off_y = OFFSETS[r]
+def neighbour(offset, sizes):
+    off_x, off_y = offset
     i, j = lax.axis_index("gx"), lax.axis_index("gy")
     return (lax.rem(i + off_x + sizes[0], sizes[0]), lax.rem(j + off_y + sizes[1], sizes[1]))
 
 
-def send(r, src, dst, sems, group, sizes):
+def send(offset, src, dst, sems, group, sizes):
     pltpu.make_async_remote_copy(
         src_ref=src,
         dst_ref=dst,
         send_sem=sems[0].at[group],
         recv_sem=sems[1].at[group],
-        device_id=neighbour(r, sizes),
+        device_id=neighbour(offset, sizes),
         device_id_type=MESH,
     ).start()
 
@@ -43,7 +45,7 @@
         dst_ref=everything,
         send_sem=sems[0].at[group],
         recv_sem=sems[1].at[group],
-        device_id=neighbour(0, sizes),
+        device_id=neighbour(OFFSETS[0], sizes),
         device_id_type=MESH,
     )
 
@@ -86,41 +88,65 @@
     return high, (value - high.astype(jnp.float32)).astype(jnp.bfloat16)
 
 
-def sample(section, dims, head, cell, plane_ref):
-    cx, cy = dims
-    inner = cx * cy
-    depth = plane_ref.shape[0] // 3
-    block = head.shape[1]
-    wx, wx_low, wx_high = cell_weights(cx, cell[0:1], head[0:1])
-    wy, wy_low, wy_high = cell_weights(cy, cell[1:2], head[1:2])
-    wz, _, _ = cell_weights(depth, cell[2:3], head[2:3])
-    own = jnp.concatenate([wx[x : x + 1] * wy for x in range(cx)], axis=0)
-    rim = [wx_high * wy, wx_low * wy, wx * wy_high, wx * wy_low]
-    rim += [wx_high * wy_high, wx_low * wy_low, wx_high * wy_low, wx_low * wy_high]
-    rim += [jnp.zeros((LANES - 2 * cx - 2 * cy - 4, block), jnp.float32)]
-    own_high, own_low = halves(own)
-    rim = jnp.concatenate(halves(jnp.concatenate(rim, axis=0)), axis=0)
-    inside = plane_ref[:, 0:inner]
-    columns = jnp.dot(inside, own_high, preferred_element_type=jnp.float32)
-    columns = columns + jnp.dot(inside, own_low, preferred_element_type=jnp.float32)
-    columns = columns + jnp.dot(plane_ref[:, inner:], rim, preferred_element_type=jnp.float32)
-    speed = jnp.concatenate(
+def sum_depth(columns, wz):
+    depth = wz.shape[0]
+    return jnp.concatenate(
         [jnp.sum(columns[k * depth : (k + 1) * depth] * wz, axis=0, keepdims=True) for k in range(3)],
         axis=0,
     )
+
+
+def multiply(plane, parts):
+    total = jnp.dot(plane, parts[0], preferred_element_type=jnp.float32)
+    for part in parts[1:]:
+        total = total + jnp.dot(plane, part, preferred_element_type=jnp.float32)
+    return total
+
+
+def own_weights(wx, wy):
+    return jnp.concatenate([wx[x : x + 1] * wy for x in range(wx.shape[0])], axis=0)
+
+
+def rim_weights(wxs, wys):
+    wx, wx_low, wx_high = wxs
+    wy, wy_low, wy_high = wys
+    rim = [wx_high * wy, wx_low * wy, wx * wy_high, wx * wy_low]
+    rim += [wx_high * wy_high, wx_low * wy_low, wx_high * wy_low, wx_low * wy_high]
+    filled = sum(part.shape[0] for part in rim)
+    rim += [jnp.zeros((LANES - filled, wy.shape[1]), jnp.float32)]
+    return jnp.concatenate(halves(jnp.concatenate(rim, axis=0)), axis=0)
+
+
+def weights_of(dims, depth, head, cell):
+    wxs = cell_weights(dims[0], cell[0:1], head[0:1])
+    wys = cell_weights(dims[1], cell[1:2], head[1:2])
+    wz, _, _ = cell_weights(depth, cell[2:3], head[2:3])
+    return wxs, wys, wz
+
+
+def advance(section, head, speed):
     moved = head[0:3] + GAMMA[section] * speed + ZETA[section] * head[3:6]
-    return jnp.concatenate([moved, speed, jnp.ones((2, block), jnp.float32)], axis=0)
+    return jnp.concatenate([moved, speed, jnp.ones((2, speed.shape[1]), jnp.float32)], axis=0)
+
+
+def sample(section, dims, head, cell, plane_ref):
+    inner = dims[0] * dims[1]
+    wxs, wys, wz = weights_of(dims, plane_ref.shape[0] // 3, head, cell)
+    columns = multiply(plane_ref[:, 0:inner], halves(own_weights(wxs[0], wys[0])))
+    columns = columns + multiply(plane_ref[:, inner:], [rim_weights(wxs, wys)])
+    return advance(section, head, sum_depth(columns, wz))
+
+
+def unpack_cell(word):
+    return jnp.concatenate([(word & 63) - 1, ((word >> 6) & 63) - 1, word >> 12], axis=0)
 
 
 def sample_all(section, dims, cells_ref, head_ref, plane_ref):
     block = BLOCK
 
-    def body(step, carry):
-        span = pl.ds(pl.multiple_of(step * block, block), block)
+    for step in range(head_ref.shape[1] // block):
+        span = slice(step * block, (step + 1) * block)
         head_ref[:, span] = sample(section, dims, head_ref[:, span], cells_ref[section, :, span], plane_ref)
-        return carry
-
-    lax.fori_loop(0, head_ref.shape[1] // block, body, 0)
 
 
 def gather_rows(index_ref, source_ref, target_ref):
@@ -188,18 +214,64 @@
         plane_ref[pl.ds(k * depth, depth), 0:inner] = own.T
 
 
-def build_rim(section, dims, halo_ref, corner_ref, plane_ref):
-    inner = dims[0] * dims[1]
+def build_rim(section, dims, halo_ref, corner_ref, plane_ref, with_plus=True):
+    cx, cy = dims
+    inner = cx * cy
     depth = halo_ref.shape[2]
     for k in range(3):
         f = 3 * section + k
         group, line = (0, f) if f < 3 else (1, f - 3)
-        faces = halo_ref[f].astype(jnp.float32)
-        corners = [corner_ref[group, d, line : line + 1, :] for d in range(4)]
-        filler = jnp.zeros((LANES - faces.shape[0] - 4, depth), jnp.float32)
-        edge = jnp.concatenate([faces] + corners + [filler], axis=0).T.astype(jnp.bfloat16)
+        plus = halo_ref[f, 0:cy, :].astype(jnp.float32) if with_plus else jnp.zeros((cy, depth), jnp.float32)
+        faces = [plus, halo_ref[f, cy:, :].astype(jnp.float32)]
+        corners = [corner_ref[group, CORNER_SLOT[d], line : line + 1, :] for d in range(4)]
+        if not with_plus:
+            corners = [jnp.zeros((1, depth), jnp.float32) if d % 2 == 0 else corners[d] for d in range(4)]
+        filler = jnp.zeros((LANES - 2 * cx - 2 * cy - 4, depth), jnp.float32)
+        edge = jnp.concatenate(faces + corners + [filler], axis=0).T.astype(jnp.bfloat16)
         plane_ref[pl.ds(k * depth, depth), inner : inner + LANES] = edge
         plane_ref[pl.ds(k * depth, depth), inner + LANES :] = edge
+
+
+def build_columns(dims, v_ref, face_ref, far_ref, column_ref):
+    cx, cy = dims
+    depth = v_ref.shape[3]
+    for k in range(3):
+        edge = []
+        for side, x, above, below in ((0, 0, 1, 3), (1, cx - 1, 2, 0)):
+            edge += [face_ref[1, side, k].astype(jnp.float32), v_ref[k, x].astype(jnp.float32)]
+            edge += [face_ref[0, side, k].astype(jnp.float32), far_ref[0, above, k : k + 1, :]]
+            edge += [jnp.zeros((LANES // 2 - 3 * cy - 2, depth), jnp.float32), far_ref[1, below, k : k + 1, :]]
+        edge = jnp.concatenate(edge, axis=0).T.astype(jnp.bfloat16)
+        column_ref[pl.ds(k * depth, depth), 0:LANES] = edge
+        column_ref[pl.ds(k * depth, depth), LANES:] = edge
+
+
+def finish_arrivals(dims, came, cap, column_ref, done_ref):
+    cx, cy = dims
+    half = LANES // 2
+    crossed = [c for c in range(len(came)) if c != 1]
+    head = jnp.concatenate([came[c] for c in crossed], axis=1)
+    cell = unpack_cell(head[6:7].astype(jnp.int32))
+    lanes = lax.broadcasted_iota(jnp.int32, (1, head.shape[1]), 1)
+    odd = (lanes & cap) > 0
+    shift = jnp.zeros((1, head.shape[1]), jnp.int32)
+    for place, c in enumerate(crossed):
+        for r in (2 * c, 2 * c + 1):
+            here = (lanes >> 6) == 2 * place + r % 2
+            shift = jnp.where(here, -cy * OFFSETS[r][1], shift)
+    wx = jnp.where(odd, jnp.where(cell[0:1] == -1, 1.0 - head[0:1], 0.0), jnp.where(cell[0:1] == cx - 1, head[0:1], 0.0))
+    base = jnp.where(odd, half, 0)
+    first = base + ((cell[1:2] + shift + cy) & (half - 1))
+    second = base + ((cell[1:2] + shift + cy + 1) & (half - 1))
+    spots = lax.broadcasted_iota(jnp.int32, (LANES, head.shape[1]), 0)
+    low, high = wx * (1.0 - head[1:2]), wx * head[1:2]
+    weight = jnp.where(spots == first, low, jnp.where(spots == second, high, 0.0))
+    wz, _, _ = cell_weights(column_ref.shape[0] // 3, cell[2:3], head[2:3])
+    columns = multiply(column_ref[...], [jnp.concatenate(halves(weight), axis=0)])
+    speed = head[3:6] + sum_depth(columns, wz)
+    for place, c in enumerate(crossed):
+        done_ref[c] = advance(0, tile(head, place), tile(speed, place))
+    done_ref[1] = advance(0, came[1], came[1][3:6])
 
 
 def plan(section, cap, count, slots_ref, counts_ref):
@@ -257,6 +329,11 @@
     away_ref,
     halo_ref,
     corner_ref,
+    face_ref,
+    far_ref,
+    column_ref,
+    done_ref,
+    late_ref,
     head_out_ref,
     head_in_ref,
     local_sem,
@@ -267,6 +344,7 @@
     sections, _, count = cells_ref.shape
     cx, cy = v_ref.shape[1], v_ref.shape[2]
     dims = (cx, cy)
+    inner = cx * cy
     moving = 8 * cap
     chunks = moving // LANES
     blocks = count // LANES
@@ -275,8 +353,8 @@
     widths = (cy, cy, cx, cx)
 
     barrier = pltpu.get_barrier_semaphore()
-    for r in range(8):
-        pl.semaphore_signal(barrier, inc=1, device_id=neighbour(r, sizes), device_id_type=MESH)
+    for offset in OFFSETS + FAR:
+        pl.semaphore_signal(barrier, inc=1, device_id=neighbour(offset, sizes), device_id_type=MESH)
 
     def fetch(k, src, dst):
         copy = pltpu.make_async_copy(src, dst, local_sem.at[k])
@@ -295,22 +373,35 @@
     def send_halo(group):
         span = spans[group]
         for r in range(8):
+            late = 2 if group == 0 and r in (1, 5, 7) else 0
             if r < 4:
                 off_x, off_y = OFFSETS[r]
                 src = v_ref.at[span, cx - 1 if off_x > 0 else 0] if off_x else yface_ref.at[r - 2, span]
                 dst = halo_ref.at[span, pl.ds(starts[r ^ 1], widths[r ^ 1]), :]
-                send(r, src, dst, sems, 2 * group, sizes)
+                send(OFFSETS[r], src, dst, sems, 4 * group + late, sizes)
             else:
-                src, dst = away_ref.at[group, r - 4], corner_ref.at[group, (r ^ 1) - 4]
-                send(r, src, dst, sems, 2 * group + 1, sizes)
-        faces = whole(halo_ref.at[span], sems, 2 * group, sizes)
-        corners = whole(corner_ref.at[group], sems, 2 * group + 1, sizes)
-        return [faces, corners]
+                src, dst = away_ref.at[group, r - 4], corner_ref.at[group, CORNER_SLOT[(r ^ 1) - 4]]
+                send(OFFSETS[r], src, dst, sems, 4 * group + late + 1, sizes)
+        if group:
+            faces = whole(halo_ref.at[span], sems, 4, sizes)
+            return [faces, whole(corner_ref.at[group], sems, 5, sizes)]
+        early = whole(halo_ref.at[span, pl.ds(cy, 2 * cx + cy), :], sems, 0, sizes)
+        late = whole(halo_ref.at[span, pl.ds(0, cy), :], sems, 2, sizes)
+        corners = [whole(corner_ref.at[group, pl.ds(2 * part, 2)], sems, 2 * part + 1, sizes) for part in range(2)]
+        return [early, corners[0], late, corners[1]]
+
+    def send_columns():
+        for r in (2, 3):
+            for side, x in ((0, 0), (1, cx - 1)):
+                send(OFFSETS[r], v_ref.at[spans[0], x], face_ref.at[(r ^ 1) - 2, side], sems, 6, sizes)
+        for k, offset in enumerate(FAR):
+            send(offset, away_ref.at[0], far_ref.at[1 - k], sems, 7, sizes)
+        return [whole(face_ref, sems, 6, sizes), whole(far_ref, sems, 7, sizes)]
 
     load_first.wait()
     find_edges(range(3), dims, v_ref, yface_ref, away_ref)
-    pl.semaphore_wait(barrier, 8)
-    halos = [send_halo(0)]
+    pl.semaphore_wait(barrier, len(OFFSETS + FAR))
+    halos = [send_halo(0), send_columns()]
 
     load_slots.wait()
     load_counts.wait()
@@ -351,12 +442,13 @@
         half = cap // 2
         for r in range(8):
             span = pl.ds(r * half, half)
-            send(r, packed_ref.at[section, span], arrived_ref.at[section, span], sems, 4 + section, sizes)
-        return [whole(arrived_ref.at[section], sems, 4 + section, sizes)]
+            send(OFFSETS[r], packed_ref.at[section, span], arrived_ref.at[section, span], sems, 8 + section, sizes)
+        return [whole(arrived_ref.at[section], sems, 8 + section, sizes)]
 
     load_state.wait()
     carried = [send_rows(0)]
-    build_inside(0, dims, v_ref, plane_ref.at[0])
+    for section in range(sections):
+        build_inside(section, dims, v_ref, plane_ref.at[section])
     for b in range(blocks):
         head_ref[:, b * LANES : (b + 1) * LANES] = rows_ref[b * LANES : (b + 1) * LANES, :].T[0:8]
 
@@ -368,7 +460,7 @@
         both = jnp.zeros((8, LANES), jnp.int32)
         for section in range(sections):
             spot = cells_ref[section, :, span]
-            word = (spot[0:1] + 1) + (spot[1:2] + 1) * 1024 + spot[2:3] * 1048576
+            word = (spot[0:1] + 1) + (spot[1:2] + 1) * 64 + spot[2:3] * 4096
             both = jnp.where(line == section, spread_row(word), both)
         packed.append(both)
     for c in range(chunks):
@@ -392,38 +484,69 @@
     pick_own(0)
     heads = []
     for section in range(sections):
+        group = 8 + sections + section
+        word = jnp.concatenate([there_ref[c, section : section + 1, :] for c in range(chunks)], axis=1)
+        cell = unpack_cell(word)
         if section == 0:
-            for copy in halos[0]:
+            head = jnp.concatenate([own_ref[c] for c in range(chunks)], axis=1)
+            r = lax.broadcasted_iota(jnp.int32, (1, moving), 1) // cap
+            plus = (r == 0) | (r == 4) | (r == 6)
+            minus = (r == 1) | (r == 5) | (r == 7)
+            wxs, wys, wz = weights_of(dims, v_ref.shape[3], head, cell)
+            inside = plane_ref[0, :, 0:inner]
+            columns = multiply(inside, halves(own_weights(wxs[0], wys[0])))
+            none = jnp.zeros_like(wxs[2])
+            lows = (wxs[0], jnp.where(minus, 0.0, wxs[1]), none)
+            highs = (jnp.zeros_like(wxs[0]), none, jnp.where(plus, 0.0, wxs[2]))
+            for copy in halos[0][0:2]:
+                copy.wait_recv()
+            build_rim(0, dims, halo_ref, corner_ref, plane_ref.at[0], with_plus=False)
+            columns = columns + multiply(plane_ref[0, :, inner:], [rim_weights(lows, wys)])
+            speed = sum_depth(columns, wz)
+            tail = [word.astype(jnp.float32), jnp.ones((1, moving), jnp.float32)]
+            message = jnp.concatenate([head[0:3], speed] + tail, axis=0)
+            for c in range(chunks):
+                head_out_ref[section, c] = tile(message, c)
+            for r in (0, 4, 6):
+                send(OFFSETS[r], head_out_ref.at[section, r // 2], head_in_ref.at[section, r], sems, group, sizes)
+            for copy in halos[0][2:4]:
                 copy.wait_recv()
             build_rim(0, dims, halo_ref, corner_ref, plane_ref.at[0])
-            leaving = [own_ref[c] for c in range(chunks)]
+            speed = speed + sum_depth(multiply(plane_ref[0, :, inner:], [rim_weights(highs, wys)]), wz)
+            message = jnp.concatenate([head[0:3], speed] + tail, axis=0)
+            for c in range(chunks):
+                late_ref[c] = tile(message, c)
+            for r in (1, 5, 7, 2, 3):
+                send(OFFSETS[r], late_ref.at[r // 2], head_in_ref.at[section, r], sems, group, sizes)
         else:
             for copy in heads[section - 1]:
                 copy.wait_recv()
             came = arrivals(section - 1)
+            if section == 1:
+                finish_arrivals(dims, came, cap, column_ref, done_ref)
+                came = [done_ref[c] for c in range(chunks)]
             leaving = [
                 select_lanes(came, spread_row(from_ref[section, c : c + 1, :]), own_ref[c]) for c in range(chunks)
             ]
-        word = jnp.concatenate([there_ref[c, section : section + 1, :] for c in range(chunks)], axis=1)
-        spot = jnp.concatenate([(word & 1023) - 1, ((word >> 10) & 1023) - 1, word >> 20], axis=0)
-        leaving = sample(section, dims, jnp.concatenate(leaving, axis=1), spot, plane_ref.at[section])
-        for c in range(chunks):
-            head_out_ref[section, c] = tile(leaving, c)
-        group = 4 + sections + section
-        for r in range(8):
-            send(r, head_out_ref.at[section, r // 2], head_in_ref.at[section, r], sems, group, sizes)
+            leaving = sample(section, dims, jnp.concatenate(leaving, axis=1), cell, plane_ref.at[section])
+            for c in range(chunks):
+                head_out_ref[section, c] = tile(leaving, c)
+            for r in range(8):
+                send(OFFSETS[r], head_out_ref.at[section, r // 2], head_in_ref.at[section, r], sems, group, sizes)
         heads.append([whole(head_in_ref.at[section], sems, group, sizes)])
 
         if section:
-            place_arrivals(section - 1, arrivals(section - 1), inverse_ref, head_ref)
+            came = [done_ref[c] for c in range(chunks)] if section == 1 else arrivals(section - 1)
+            place_arrivals(section - 1, came, inverse_ref, head_ref)
         sample_all(section, dims, cells_ref, head_ref, plane_ref.at[section])
         if section + 1 < sections:
             pick_own(section + 1)
-            build_inside(section + 1, dims, v_ref, plane_ref.at[section + 1])
             if section == 0:
-                for copy in halos[1]:
+                for copy in halos[1] + halos[2]:
                     copy.wait_recv()
-            build_rim(section + 1, dims, halo_ref, corner_ref, plane_ref.at[section + 1])
+                build_columns(dims, v_ref, face_ref, far_ref, column_ref)
+                for later in range(1, sections):
+                    build_rim(later, dims, halo_ref, corner_ref, plane_ref.at[later])
             for copy in carried[section]:
                 copy.wait_recv()
             decode_rows(arrived_ref.at[section], rows_ref, count + section * moving)
@@ -521,11 +644,16 @@
             pltpu.VMEM((2, 4, 8, depth), jnp.float32),
             pltpu.VMEM((fields, rim, depth), field.dtype),
             pltpu.VMEM((2, 4, 8, depth), jnp.float32),
+            pltpu.VMEM((2, 2, 3, cy, depth), field.dtype),
+            pltpu.VMEM((2, 4, 8, depth), jnp.float32),
+            pltpu.VMEM((3 * depth, 2 * LANES), jnp.bfloat16),
+            pltpu.VMEM((chunks, 8, LANES), jnp.float32),
+            pltpu.VMEM((chunks, 8, LANES), jnp.float32),
             pltpu.VMEM((sections, chunks, 8, LANES), jnp.float32),
             pltpu.VMEM((sections, 8, 8, LANES), jnp.float32),
             pltpu.SemaphoreType.DMA((7 + sections,)),
-            pltpu.SemaphoreType.DMA((4 + 2 * sections,)),
-            pltpu.SemaphoreType.DMA((4 + 2 * sections,)),
+            pltpu.SemaphoreType.DMA((8 + 2 * sections,)),
+            pltpu.SemaphoreType.DMA((8 + 2 * sections,)),
         ],
         compiler_params=pltpu.CompilerParams(collective_id=0, has_side_effects=True),
     )(state, field, cells, slots, counts)

time: 27.6 us -> 25.8 us (0.935); the launches traced: 27.1 us -> 25.6 us
  Pallas kernels: 27.1 us -> 25.6 us
    pallas_call x1, Pallas kernels: 25.7 us -> 24.2 us  [local(): pl.pallas_call(functools.partial(steps_kernel, sizes, cap), out_shape=(pl...]
where the time goes in v3:
time: 25.8 us; the launch traced here: 25.6 us
  Pallas kernels  25.6 us (99%)
    pallas_call x1, Pallas kernels, local(): pl.pallas_call(functools.partial(steps_kernel, sizes, cap), out_shape=(pl...  24.2 us
    pallas_call x1, Pallas kernels, local(): pl.pallas_call(functools.partial(last_kernel, cap), out_shape=jax.ShapeDt...  1.47 us

profile of v3, /device:TPU:0, one launch (start us, length us, event | category | flops | bytes accessed | tf_op | source)
XLA Modules:
  0.0 25.6 jit_solution(13472060094421364372)
XLA Ops:
  0.0 24.2 %shard_map.55 = (f32[2048,128]{1,0:T(8,128)S(1)}, f32[512,128]{1,0:T(8,128)S(1)}, s32[3,8,128]{2,1,0:T(8,128)S(4)}, s32[3,1,1,8]{3,2,1,0:T(1,128)S(4)}, s32[16,128]{1,0:T(8,128)S(4)}) custom-call(f32[2048,128]{1,0:T(8,128)} %state_hbm.1, bf16[9,16,16,128]{3,2,1,0:T(8,128)(2,1)} %bitcast.1, s32[3,3,2048]{2,1,0:T(4,128)} %cells_hbm.1, s32[3,2048]{1,0:T(4,128)} %slots_hbm.1, ...), custom_call_target="tpu_custom_call" | custom-call | tf_op jit(solution)/shard_map/pallas_call | solution.py:616
  24.2 1.5 %shard_map.56 = f32[2048,128]{1,0:T(8,128)} custom-call(f32[2048,128]{1,0:T(8,128)S(1)} %get-tuple-element.8.base_ref, f32[512,128]{1,0:T(8,128)S(1)} %get-tuple-element.9.merged_ref, s32[3,8,128]{2,1,0:T(8,128)S(4)} %get-tuple-element.10.index_ref), custom_call_target="tpu_custom_call" | custom-call | tf_op jit(solution)/shard_map/pallas_call | solution.py:662

commit v4 on v3

--- a/solution.py
+++ b/solution.py
@@ -150,12 +150,8 @@
 
 
 def gather_rows(index_ref, source_ref, target_ref):
-    def body(row, carry):
-        for u in range(LANES):
-            target_ref[pl.ds(row * LANES + u, 1), :] = source_ref[pl.ds(index_ref[row, u], 1), :]
-        return carry
-
-    lax.fori_loop(0, target_ref.shape[0] // LANES, body, 0)
+    for t in range(target_ref.shape[0]):
+        target_ref[t : t + 1, :] = source_ref[pl.ds(index_ref[t // LANES, t % LANES], 1), :]
 
 
 def encode(rows):
@@ -307,6 +303,7 @@
     counts_hbm,
     base_ref,
     merged_ref,
+    goal_ref,
     index_ref,
     counts_ref,
     places_ref,
@@ -426,6 +423,7 @@
         if section + 1 == sections:
             final_ref[...] = jnp.clip(table, 0, count + section * moving - 1)
             places.append(fetch(6 + sections, final_ref, places_ref))
+            places.append(fetch(7 + sections, staged_ref.at[section], goal_ref))
         table = jnp.where(inverse > 0, inverse + (count + section * moving - 1), table)
         inverse_ref[section] = inverse - 1
         slots.append(slot)
@@ -553,6 +551,7 @@
             carried.append(send_rows(section + 1))
 
     places[sections].wait()
+    places[sections + 1].wait()
     gather_rows(places_ref, rows_ref, base_ref)
     for b in range(blocks):
         span = slice(b * LANES, (b + 1) * LANES)
@@ -585,19 +584,14 @@
         head_ref[:, span] = select_lanes(came, where_, head_ref[:, span])
 
 
-def last_kernel(cap, base_ref, merged_ref, index_ref, out_hbm, final_ref, sem):
+def last_kernel(cap, base_ref, merged_ref, goal_ref, out_hbm, final_ref, sem):
     count = out_hbm.shape[0]
-    last = index_ref.shape[0] - 1
     chunks = 8 * cap // LANES
     final_ref[0:count, :] = base_ref[...]
 
-    def body(row, carry):
-        for u in range(LANES):
-            goal = index_ref[last, chunks + row, u]
-            final_ref[pl.ds(goal, 1), :] = merged_ref[pl.ds(row * LANES + (u ^ cap), 1), :]
-        return carry
-
-    lax.fori_loop(0, chunks, body, 0)
+    for t in range(8 * cap):
+        goal = goal_ref[chunks + t // LANES, t % LANES]
+        final_ref[pl.ds(goal, 1), :] = merged_ref[(t ^ cap) : (t ^ cap) + 1, :]
     copy = pltpu.make_async_copy(final_ref.at[pl.ds(0, count)], out_hbm, sem)
     copy.start()
     copy.wait()
@@ -613,18 +607,19 @@
     inner = cx * cy
     rim = 2 * cx + 2 * cy
     half = moving // 2
-    base, merged, index, _, _ = pl.pallas_call(
+    base, merged, goal = pl.pallas_call(
         functools.partial(steps_kernel, sizes, cap),
         out_shape=(
             pltpu.VMEM((count, width), jnp.float32),
             pltpu.VMEM((moving, width), jnp.float32),
+            pltpu.SMEM((2 * chunks, LANES), jnp.int32),
+        ),
+        in_specs=[ANY] * 5,
+        out_specs=(VMEM, VMEM, SMEM),
+        scratch_shapes=[
             pltpu.SMEM((sections, 2 * chunks, LANES), jnp.int32),
             pltpu.SMEM(counts.shape, jnp.int32),
             pltpu.SMEM((count // LANES, LANES), jnp.int32),
-        ),
-        in_specs=[ANY] * 5,
-        out_specs=(VMEM, VMEM, SMEM, SMEM, SMEM),
-        scratch_shapes=[
             pltpu.VMEM((count + (sections - 1) * moving, width), jnp.float32),
             pltpu.VMEM((sections, half, width), jnp.int32),
             pltpu.VMEM((sections, half, width), jnp.int32),
@@ -651,21 +646,21 @@
             pltpu.VMEM((chunks, 8, LANES), jnp.float32),
             pltpu.VMEM((sections, chunks, 8, LANES), jnp.float32),
             pltpu.VMEM((sections, 8, 8, LANES), jnp.float32),
-            pltpu.SemaphoreType.DMA((7 + sections,)),
+            pltpu.SemaphoreType.DMA((8 + sections,)),
             pltpu.SemaphoreType.DMA((8 + 2 * sections,)),
             pltpu.SemaphoreType.DMA((8 + 2 * sections,)),
         ],
         compiler_params=pltpu.CompilerParams(collective_id=0, has_side_effects=True),
     )(state, field, cells, slots, counts)
     base, merged = (pltpu.with_memory_space_constraint(x, pltpu.VMEM) for x in (base, merged))
-    index = pltpu.with_memory_space_constraint(index, pltpu.SMEM)
+    goal = pltpu.with_memory_space_constraint(goal, pltpu.SMEM)
     return pl.pallas_call(
         functools.partial(last_kernel, cap),
         out_shape=jax.ShapeDtypeStruct((count, width), jnp.float32),
         in_specs=[VMEM, VMEM, SMEM],
         out_specs=ANY,
         scratch_shapes=[pltpu.VMEM((count + SPARE, width), jnp.float32), pltpu.SemaphoreType.DMA],
-    )(base, merged, index)
+    )(base, merged, goal)
 
 
 def solution(mesh):

time: 25.8 us -> 25.4 us (0.984)
  Pallas kernels: 25.6 us -> 25.2 us
    pallas_call x1, Pallas kernels: 24.2 us -> 23.8 us  [local(): pl.pallas_call(functools.partial(steps_kernel, sizes, cap), out_shape=(pl...]
where the time goes in v4:
time: 25.4 us; the launch traced here: 25.2 us
  Pallas kernels  25.2 us (99%)
    pallas_call x1, Pallas kernels, local(): pl.pallas_call(functools.partial(steps_kernel, sizes, cap), out_shape=(pl...  23.8 us
    pallas_call x1, Pallas kernels, local(): pl.pallas_call(functools.partial(last_kernel, cap), out_shape=jax.ShapeDt...  1.45 us

profile of v4, /device:TPU:0, one launch (start us, length us, event | category | flops | bytes accessed | tf_op | source)
XLA Modules:
  0.0 25.2 jit_solution(7654376011619723139)
XLA Ops:
  0.0 23.8 %shard_map.55 = (f32[2048,128]{1,0:T(8,128)S(1)}, f32[512,128]{1,0:T(8,128)S(1)}, s32[8,128]{1,0:T(8,128)S(4)}) custom-call(f32[2048,128]{1,0:T(8,128)} %state_hbm.1, bf16[9,16,16,128]{3,2,1,0:T(8,128)(2,1)} %bitcast.1, s32[3,3,2048]{2,1,0:T(4,128)} %cells_hbm.1, s32[3,2048]{1,0:T(4,128)} %slots_hbm.1, s32[3,1,1,8]{3,2,1,0:T(1,128)} %counts_hbm.1), custom_call_target="tpu_custom_call" | custom-call | tf_op jit(solution)/shard_map/pallas_call | solution.py:610
  23.8 1.4 %shard_map.56 = f32[2048,128]{1,0:T(8,128)} custom-call(f32[2048,128]{1,0:T(8,128)S(1)} %get-tuple-element.8.base_ref, f32[512,128]{1,0:T(8,128)S(1)} %get-tuple-element.9.merged_ref, s32[8,128]{1,0:T(8,128)S(4)} %get-tuple-element.10.goal_ref), custom_call_target="tpu_custom_call" | custom-call | tf_op jit(solution)/shard_map/pallas_call | solution.py:657
